TPU v7x, 32 devices: a whole 2x2x4 slice. The times are simulated.
32 devices in a mesh: region: 8 (over z, y), blk: 4 (over x, core).
Axes of the slice: x: 2, y: 2, z: 4, core: 2. Of those that a mesh axis runs over, the one named last changes fastest.
Arguments:
- jac_bus: float32 [256, 8, 128, 128], P('region', 'blk'), may hold values from -0.1875 to 0.1875
- pattern: int32 [256, 8], P(('region', 'blk')), may hold values from 0 to 23
- branch_weight: float32 [256, 128], P(('region', 'blk')), may hold values from 0.2 to 5
- bus_diag: float32 [256, 128], P(('region', 'blk')), may hold values from 0.3 to 3
- right_side: float32 [256, 128], P(('region', 'blk')), may hold values from -8 to 8
Outputs:
- solution: float32 [256, 128], P(('region', 'blk'))
- residual: float32 [256, 128], P(('region', 'blk'))
Inputs may be any that keep to these rules, and one draw needn't show every extreme that they name: pattern values below 8 name the region before the branch tile's region, those from 16 the region after it, with regions closed into a loop.
All inputs are finite; a program needn't handle non-finite values.
Results may differ from a plain program's by a relative error of at most 0.0003.
Values sent between devices are 32-bit elements; how exact they have to be, the bound alone decides.
No kernel may reach another device: no remote copies, remote signals or barrier semaphores. Data moves between devices by JAX's collectives and lax.ppermute only.
A program may use at most 64 MiB of HBM per device.

v0:
```python
import jax
import jax.numpy as jnp
from jax import lax
from jax.sharding import PartitionSpec as P

ITERS = 12


def extended(array, sides, width):
    for axis, dim in sides:
        size, length = (lax.axis_size(axis), array.shape[dim])
        up = [(i, (i + 1) % size) for i in range(size)]
        down = [(j, i) for i, j in up]
        last = lax.slice_in_dim(array, length - width, length, axis=dim)
        leading = lax.slice_in_dim(array, 0, width, axis=dim)
        before = lax.ppermute(last, axis, up)
        after = lax.ppermute(leading, axis, down)
        array = jnp.concatenate([before, array, after], axis=dim)
    return array


def from_behind(array, axis, by):
    length = lax.axis_size(axis)
    return lax.ppermute(array, axis, [(i, (i + by) % length) for i in range(length)])


def neighbours(values):
    return extended(values[None], (("region", 0),), 1)


def route(lower, middle, upper):
    from_upper = from_behind(lower, "region", -1)
    from_lower = from_behind(upper, "region", 1)
    return middle + from_upper + from_lower


def spread(tiles, weight, index, count):
    back = jnp.einsum("tjab,ta->tjb", tiles, weight, precision=lax.Precision.HIGHEST)
    width = back.shape[-1]
    return jnp.zeros((count, width), jnp.float32).at[index.reshape(-1)].add(back.reshape(-1, width))


def body(jac_bus, pattern, branch_weight, bus_diag, right_side):
    hp = lax.Precision.HIGHEST
    blocks = lax.axis_size("blk")
    per_dev = right_side.shape[0]
    width = right_side.shape[1]
    group_len = jac_bus.shape[1]
    tiles = lax.all_to_all(jac_bus, "blk", split_axis=0, concat_axis=1, tiled=True)
    group = jnp.arange(tiles.shape[1], dtype=jnp.int32) // group_len
    index = pattern // per_dev * (blocks * per_dev) + group[None, :] * per_dev + pattern % per_dev

    def collect(buffer):
        parts = buffer.reshape(3, blocks, per_dev, width)
        total = route(parts[0], parts[1], parts[2])
        return lax.psum_scatter(total, "blk", scatter_dimension=0, tiled=True)[0]

    def branch_rows(vector):
        region_vals = lax.all_gather(vector[None], "blk", axis=0, tiled=True)
        flat = neighbours(region_vals).reshape(-1, width)
        return jnp.einsum("tjab,tjb->ta", tiles, flat[index], precision=hp)

    count = 3 * blocks * per_dev

    def apply_operator(vector):
        rows = branch_rows(vector)
        return bus_diag * vector + collect(spread(tiles, branch_weight * rows, index, count))

    precond = bus_diag + collect(spread(tiles * tiles, branch_weight, index, count))
    solution = jnp.zeros_like(right_side)
    residual = right_side

    def paired(resid):
        scaled = resid / precond
        image = apply_operator(scaled)
        gamma, delta = lax.psum(
            (jnp.sum(resid * scaled), jnp.sum(image * scaled)), ("region", "blk")
        )
        return (scaled, image, gamma, delta)

    scaled, image, gamma, delta = paired(residual)
    alpha = gamma / delta
    direction, along = (scaled, image)
    solution = alpha * direction
    residual = residual - alpha * along

    def one_step(step, carry):
        solution, residual, direction, along, gamma, alpha = carry
        scaled, image, fresh, delta = paired(residual)
        beta = fresh / gamma
        alpha = fresh / (delta - beta * fresh / alpha)
        direction = scaled + beta * direction
        along = image + beta * along
        solution = solution + alpha * direction
        residual = residual - alpha * along
        return (solution, residual, direction, along, fresh, alpha)

    carry = lax.fori_loop(
        0, ITERS - 1, one_step, (solution, residual, direction, along, gamma, alpha)
    )
    solution, residual = (carry[0], carry[1])
    return (solution, residual)


def solution(mesh):
    return jax.shard_map(
        body,
        mesh=mesh,
        in_specs=(
            P("region", "blk", None, None),
            P(("region", "blk"), None),
            P(("region", "blk"), None),
            P(("region", "blk"), None),
            P(("region", "blk"), None),
        ),
        out_specs=(P(("region", "blk"), None), P(("region", "blk"), None)),
        check_vma=False,
    )
```

profile of v0, /device:TPU:14, one launch (start us, length us, event | category | flops | bytes accessed | tf_op | source)
XLA Modules:
  0.0 1099.4 jit_solution(10616008818148607382)
XLA Ops:
  0.6 5.4 all-to-all-start
  6.1 46.5 %all-to-all-done = f32[32,2,128,128]{3,2,1,0:T(8,128)} async-done(((f32[32,2,128,128]{3,2,1,0:T(8,128)}), f32[32,2,128,128]{3,2,1,0:T(8,128)}, u32[]{:S(2)}, u32[]{:S(2)}) %all-to-all-start) | async-done | bytes 4194336 | tf_op jit(solution)/shard_map/all_to_all | solution.py:49
  64.9 10.1 all-reduce.1
  75.7 5.2 all-gather.1
  89.1 5.4 fusion.33
  102.3 10.1 all-reduce.2
  113.6 51.1 %all-reduce.4 = (f32[]{:T(128)}, f32[]{:T(128)}) all-reduce(f32[]{:T(128)} %get-tuple-element.70, f32[]{:T(128)} %get-tuple-element.69), channel_id=1, replica_groups=mesh['region'=8,'blk'=4] {'region','blk'}, use_global_device_ids=true, to_apply=%region_3.4 | all-reduce | flops 2 | bytes 16 | tf_op jit(solution)/shard_map/psum | solution.py:76
  166.0 932.8 %while.21 = (s32[]{:T(128)}, f32[8,128]{1,0:T(8,128)S(1)}, f32[8,128]{1,0:T(8,128)S(1)}, f32[8,128]{1,0:T(8,128)S(1)}, f32[8,128]{1,0:T(8,128)S(1)}, /*index=5*/...) while((s32[]{:T(128)}, f32[8,128]{1,0:T(8,128)S(1)}, ...), condition=%wide.wide.region_15.16_spmd, body=%wide.wide.region_8.15_spmd.sunk | while | flops 25230720 | bytes 25991660 | solution.py:98
  166.0 5.2 all-gather.4
  177.0 5.4 fusion.68
  192.4 10.1 all-reduce.9
  203.8 44.6 %all-reduce.10 = (f32[]{:T(128)}, f32[]{:T(128)}) all-reduce(f32[]{:T(128)} %get-tuple-element.267, f32[]{:T(128)} %get-tuple-element.268), channel_id=1, replica_groups=mesh['region'=8,'blk'=4] {'region','blk'}, use_global_device_ids=true, to_apply=%region_10.10 | all-reduce | flops 2 | bytes 16 | tf_op jit(solution)/shard_map/while/body/eval_jaxpr/psum | solution.py:76
  251.4 5.2 all-gather.4
  261.8 5.4 fusion.68
  277.8 10.1 all-reduce.9
  289.2 43.4 %all-reduce.10 = (f32[]{:T(128)}, f32[]{:T(128)}) all-reduce(f32[]{:T(128)} %get-tuple-element.267, f32[]{:T(128)} %get-tuple-element.268), channel_id=1, replica_groups=mesh['region'=8,'blk'=4] {'region','blk'}, use_global_device_ids=true, to_apply=%region_10.10 | all-reduce | flops 2 | bytes 16 | tf_op jit(solution)/shard_map/while/body/eval_jaxpr/psum | solution.py:76
  335.5 5.2 all-gather.4
  346.5 5.4 fusion.68
  361.9 10.1 all-reduce.9
  373.3 44.6 %all-reduce.10 = (f32[]{:T(128)}, f32[]{:T(128)}) all-reduce(f32[]{:T(128)} %get-tuple-element.267, f32[]{:T(128)} %get-tuple-element.268), channel_id=1, replica_groups=mesh['region'=8,'blk'=4] {'region','blk'}, use_global_device_ids=true, to_apply=%region_10.10 | all-reduce | flops 2 | bytes 16 | tf_op jit(solution)/shard_map/while/body/eval_jaxpr/psum | solution.py:76
  420.9 5.2 all-gather.4
  431.3 5.4 fusion.68
  447.3 10.1 all-reduce.9
  458.7 43.4 %all-reduce.10 = (f32[]{:T(128)}, f32[]{:T(128)}) all-reduce(f32[]{:T(128)} %get-tuple-element.267, f32[]{:T(128)} %get-tuple-element.268), channel_id=1, replica_groups=mesh['region'=8,'blk'=4] {'region','blk'}, use_global_device_ids=true, to_apply=%region_10.10 | all-reduce | flops 2 | bytes 16 | tf_op jit(solution)/shard_map/while/body/eval_jaxpr/psum | solution.py:76
  505.0 5.2 all-gather.4
  516.0 5.4 fusion.68
  531.4 10.1 all-reduce.9
  542.8 44.6 %all-reduce.10 = (f32[]{:T(128)}, f32[]{:T(128)}) all-reduce(f32[]{:T(128)} %get-tuple-element.267, f32[]{:T(128)} %get-tuple-element.268), channel_id=1, replica_groups=mesh['region'=8,'blk'=4] {'region','blk'}, use_global_device_ids=true, to_apply=%region_10.10 | all-reduce | flops 2 | bytes 16 | tf_op jit(solution)/shard_map/while/body/eval_jaxpr/psum | solution.py:76
  600.8 5.4 fusion.68
  616.7 10.1 all-reduce.9
  628.1 43.4 %all-reduce.10 = (f32[]{:T(128)}, f32[]{:T(128)}) all-reduce(f32[]{:T(128)} %get-tuple-element.267, f32[]{:T(128)} %get-tuple-element.268), channel_id=1, replica_groups=mesh['region'=8,'blk'=4] {'region','blk'}, use_global_device_ids=true, to_apply=%region_10.10 | all-reduce | flops 2 | bytes 16 | tf_op jit(solution)/shard_map/while/body/eval_jaxpr/psum | solution.py:76
  685.4 5.4 fusion.68
  700.9 10.1 all-reduce.9
  712.3 44.6 %all-reduce.10 = (f32[]{:T(128)}, f32[]{:T(128)}) all-reduce(f32[]{:T(128)} %get-tuple-element.267, f32[]{:T(128)} %get-tuple-element.268), channel_id=1, replica_groups=mesh['region'=8,'blk'=4] {'region','blk'}, use_global_device_ids=true, to_apply=%region_10.10 | all-reduce | flops 2 | bytes 16 | tf_op jit(solution)/shard_map/while/body/eval_jaxpr/psum | solution.py:76
  759.8 5.2 all-gather.4
  770.3 5.4 fusion.68
  786.2 10.1 all-reduce.9
  797.6 43.4 %all-reduce.10 = (f32[]{:T(128)}, f32[]{:T(128)}) all-reduce(f32[]{:T(128)} %get-tuple-element.267, f32[]{:T(128)} %get-tuple-element.268), channel_id=1, replica_groups=mesh['region'=8,'blk'=4] {'region','blk'}, use_global_device_ids=true, to_apply=%region_10.10 | all-reduce | flops 2 | bytes 16 | tf_op jit(solution)/shard_map/while/body/eval_jaxpr/psum | solution.py:76
  854.9 5.4 fusion.68
  870.4 10.1 all-reduce.9
  881.8 44.6 %all-reduce.10 = (f32[]{:T(128)}, f32[]{:T(128)}) all-reduce(f32[]{:T(128)} %get-tuple-element.267, f32[]{:T(128)} %get-tuple-element.268), channel_id=1, replica_groups=mesh['region'=8,'blk'=4] {'region','blk'}, use_global_device_ids=true, to_apply=%region_10.10 | all-reduce | flops 2 | bytes 16 | tf_op jit(solution)/shard_map/while/body/eval_jaxpr/psum | solution.py:76
  929.3 5.2 all-gather.4
  939.8 5.4 fusion.68
  955.7 10.1 all-reduce.9
  967.1 43.4 %all-reduce.10 = (f32[]{:T(128)}, f32[]{:T(128)}) all-reduce(f32[]{:T(128)} %get-tuple-element.267, f32[]{:T(128)} %get-tuple-element.268), channel_id=1, replica_groups=mesh['region'=8,'blk'=4] {'region','blk'}, use_global_device_ids=true, to_apply=%region_10.10 | all-reduce | flops 2 | bytes 16 | tf_op jit(solution)/shard_map/while/body/eval_jaxpr/psum | solution.py:76
  1024.4 5.4 fusion.68
  1039.8 10.1 all-reduce.9
  1051.3 44.6 %all-reduce.10 = (f32[]{:T(128)}, f32[]{:T(128)}) all-reduce(f32[]{:T(128)} %get-tuple-element.267, f32[]{:T(128)} %get-tuple-element.268), channel_id=1, replica_groups=mesh['region'=8,'blk'=4] {'region','blk'}, use_global_device_ids=true, to_apply=%region_10.10 | all-reduce | flops 2 | bytes 16 | tf_op jit(solution)/shard_map/while/body/eval_jaxpr/psum | solution.py:76
  (332 shorter events, 239.9 us)
Async XLA Ops:
  0.6 52.0 %all-to-all-start = ((f32[32,2,128,128]{3,2,1,0:T(8,128)}), f32[32,2,128,128]{3,2,1,0:T(8,128)}, u32[]{:S(2)}, u32[]{:S(2)}) async-start(f32[32,2,128,128]{3,2,1,0:T(8,128)} %param.7), calls=%async_computation | async-start | bytes 8388608 | tf_op jit(solution)/shard_map/all_to_all | solution.py:49
  60.2 4.7 collective-permute-start.4
  60.8 4.1 collective-permute-start.5
  80.9 4.4 collective-permute-start.6
  83.8 4.6 collective-permute-start.7
  97.4 4.7 collective-permute-start.8
  97.5 4.8 collective-permute-start.9
  171.2 4.6 collective-permute-start
  172.6 3.7 collective-permute-start.1
  185.3 3.9 collective-permute-start.2
  187.8 4.6 collective-permute-start.3
  256.6 4.6 collective-permute-start
  256.8 4.4 collective-permute-start.1
  270.2 4.4 collective-permute-start.2
  273.1 4.6 collective-permute-start.3
  340.7 4.6 collective-permute-start
  342.1 3.7 collective-permute-start.1
  354.8 3.9 collective-permute-start.2
  357.3 4.6 collective-permute-start.3
  426.1 4.6 collective-permute-start
  426.3 4.4 collective-permute-start.1
  439.6 4.4 collective-permute-start.2
  442.6 4.6 collective-permute-start.3
  510.2 4.6 collective-permute-start
  511.6 3.7 collective-permute-start.1
  524.3 3.9 collective-permute-start.2
  526.8 4.6 collective-permute-start.3
  595.5 4.6 collective-permute-start
  595.8 4.4 collective-permute-start.1
  609.1 4.4 collective-permute-start.2
  612.1 4.6 collective-permute-start.3
  679.7 4.6 collective-permute-start
  693.8 3.9 collective-permute-start.2
  696.2 4.6 collective-permute-start.3
  765.0 4.6 collective-permute-start
  765.2 4.4 collective-permute-start.1
  778.6 4.4 collective-permute-start.2
  781.6 4.6 collective-permute-start.3
  849.2 4.6 collective-permute-start
  863.3 3.9 collective-permute-start.2
  865.7 4.6 collective-permute-start.3
  934.5 4.6 collective-permute-start
  934.7 4.4 collective-permute-start.1
  948.1 4.4 collective-permute-start.2
  951.1 4.6 collective-permute-start.3
  1018.7 4.6 collective-permute-start
  1032.7 3.9 collective-permute-start.2
  1035.2 4.6 collective-permute-start.3
  (23 other events, 137.2 us)
where the time goes:
time: 1100 us
  blocking collectives  729 us (66%)
  waiting for transfers between devices  113 us (10%)
  matrix products  92.2 us (8%)
  starting transfers between devices  76.1 us (7%)
  other arithmetic  34 us (3%)
  loops' own time  32.3 us (3%)
  local copies, waits for them, and re-layouts  20.5 us (2%)
    psum x12, blocking collectives, paired(): lax.psum((jnp.sum(resid * scaled), jnp.sum(image * scaled)), ('region', '...  535 us
    while x11, blocking collectives  111 us
    dot_general x12, matrix products, branch_rows(): return jnp.einsum('tjab,tjb->ta', tiles, flat[index], precision=hp)  64.8 us
    all_gather x12, blocking collectives, branch_rows(): region_vals = lax.all_gather(vector[None], 'blk', axis=0, tiled=True)  62.5 us
    all_to_all x1, waiting for transfers between devices, body(): lax.all_to_all(jac_bus, 'blk', split_axis=0, concat_axis=1, tiled=True)  46.5 us
    ppermute x26, waiting for transfers between devices, from_behind(): lax.ppermute(array, axis, [(i, (i + by) % length) for i in range(length)])  41.1 us
    ppermute x26, starting transfers between devices, from_behind(): lax.ppermute(array, axis, [(i, (i + by) % length) for i in range(length)])  35.6 us
    another operation x1, loops' own time, body(): lax.fori_loop(0, ITERS - 1, one_step, (solution, residual, direction, alo...  32.3 us
  transfers between devices with their start and end apart: 51, of which 45 were waited for; matrix products, arithmetic and copies ran while one was open for 1% of the time, Pallas kernels for 0%

commit v1 on v0

--- a/solution.py
+++ b/solution.py
@@ -2,6 +2,7 @@
 import jax.numpy as jnp
 from jax import lax
 from jax.sharding import PartitionSpec as P
+from jax.lax import psum
 
 ITERS = 12
 
@@ -71,11 +72,17 @@
     residual = right_side
 
     def paired(resid):
+
+        def get_slices_for(state):
+            link_axis = "region"
+            across = "blk"
+            for u in (across, link_axis):
+                state = psum(state, u)
+            return state
+
         scaled = resid / precond
         image = apply_operator(scaled)
-        gamma, delta = lax.psum(
-            (jnp.sum(resid * scaled), jnp.sum(image * scaled)), ("region", "blk")
-        )
+        gamma, delta = get_slices_for((jnp.sum(resid * scaled), jnp.sum(image * scaled)))
         return (scaled, image, gamma, delta)
 
     scaled, image, gamma, delta = paired(residual)

time: 1100 us -> 931 us (0.85); the launches traced: 1100 us -> 919 us
  blocking collectives: 729 us -> 532 us
  starting transfers between devices: 76.1 us -> 95.6 us
    psum x12 -> x24, blocking collectives: 535 us -> 337 us  [get_slices_for(): state = psum(state, u)]
    ppermute x12, starting transfers between devices: 9.62 us -> 47.2 us  [extended(): after = lax.ppermute(leading, axis, down)]
    ppermute x12, waiting for transfers between devices: 4.52 us -> 26.2 us  [extended(): before = lax.ppermute(last, axis, up)]
    ppermute x26, waiting for transfers between devices: 41.1 us -> 20.6 us  [from_behind(): lax.ppermute(array, axis, [(i, (i + by) % length) for i in range(length)])]
    ppermute x12, starting transfers between devices: 25.5 us -> 5.83 us  [extended(): before = lax.ppermute(last, axis, up)]
  transfers between devices with their start and end apart: 51 -> 51, of which waited for: 45 -> 50; matrix products, arithmetic and copies ran while one was open for 1% -> 1% of each run, Pallas kernels for 0% -> 0%
where the time goes in v1:
time: 931 us; the launch traced here: 919 us
  blocking collectives  532 us (57%)
  waiting for transfers between devices  111 us (12%)
  starting transfers between devices  95.6 us (10%)
  matrix products  92.2 us (10%)
  other arithmetic  33.1 us (4%)
  loops' own time  32.3 us (3%)
  local copies, waits for them, and re-layouts  20.5 us (2%)
    psum x24, blocking collectives, get_slices_for(): state = psum(state, u)  337 us
    while x11, blocking collectives  111 us
    dot_general x12, matrix products, branch_rows(): return jnp.einsum('tjab,tjb->ta', tiles, flat[index], precision=hp)  64.8 us
    all_gather x12, blocking collectives, branch_rows(): region_vals = lax.all_gather(vector[None], 'blk', axis=0, tiled=True)  63.1 us
    ppermute x12, starting transfers between devices, extended(): after = lax.ppermute(leading, axis, down)  47.2 us
    all_to_all x1, waiting for transfers between devices, body(): lax.all_to_all(jac_bus, 'blk', split_axis=0, concat_axis=1, tiled=True)  46.5 us
    ppermute x26, starting transfers between devices, from_behind(): lax.ppermute(array, axis, [(i, (i + by) % length) for i in range(length)])  37.2 us
    another operation x1, loops' own time, body(): lax.fori_loop(0, ITERS - 1, one_step, (solution, residual, direction, alo...  32.3 us
  transfers between devices with their start and end apart: 51, of which 50 were waited for; matrix products, arithmetic and copies ran while one was open for 1% of the time, Pallas kernels for 0%

profile of v1, /device:TPU:14, one launch (start us, length us, event | category | flops | bytes accessed | tf_op | source)
XLA Modules:
  0.0 918.8 jit_solution(10062033673107678733)
XLA Ops:
  6.1 46.5 %all-to-all-done = f32[32,2,128,128]{3,2,1,0:T(8,128)} async-done(((f32[32,2,128,128]{3,2,1,0:T(8,128)}), f32[32,2,128,128]{3,2,1,0:T(8,128)}, u32[]{:S(2)}, u32[]{:S(2)}) %all-to-all-start) | async-done | bytes 4194336 | tf_op jit(solution)/shard_map/all_to_all | solution.py:50
  64.9 10.1 %all-reduce.1 = f32[4,8,128]{2,1,0:T(8,128)S(1)} all-reduce(f32[4,8,128]{2,1,0:T(8,128)S(1)} %fusion.15), channel_id=5, replica_groups=mesh['region'=8,'blk'=4] {'blk'}, use_global_device_ids=true, to_apply=%region_1.2.clone | all-reduce | flops 4096 | bytes 32768
  89.1 5.4 fusion.33
  102.3 10.1 %all-reduce.2 = f32[4,8,128]{2,1,0:T(8,128)S(1)} all-reduce(f32[4,8,128]{2,1,0:T(8,128)S(1)} %fusion.13), channel_id=6, replica_groups=mesh['region'=8,'blk'=4] {'blk'}, use_global_device_ids=true, to_apply=%region_6.7.clone | all-reduce | flops 4096 | bytes 32768
  113.7 6.3 all-reduce.6
  119.9 27.2 %all-reduce.5 = (f32[]{:T(128)}, f32[]{:T(128)}) all-reduce(f32[]{:T(128)} %get-tuple-element.101, f32[]{:T(128)} %get-tuple-element.102), channel_id=1, replica_groups=mesh['region'=8,'blk'=4] {'region'}, use_global_device_ids=true, to_apply=%region_4.5 | all-reduce | flops 2 | bytes 16 | tf_op jit(solution)/shard_map/psum | solution.py:80
  148.4 769.8 %while.21 = (s32[]{:T(128)}, f32[8,128]{1,0:T(8,128)S(1)}, f32[8,128]{1,0:T(8,128)S(1)}, f32[8,128]{1,0:T(8,128)S(1)}, f32[8,128]{1,0:T(8,128)S(1)}, /*index=5*/...) while((s32[]{:T(128)}, f32[8,128]{1,0:T(8,128)S(1)}, ...), condition=%wide.wide.region_19.20_spmd, body=%wide.wide.region_10.19_spmd.sunk | while | flops 25230724 | bytes 25991676 | solution.py:105
  174.8 10.1 %all-reduce.13 = f32[4,8,128]{2,1,0:T(8,128)S(1)} all-reduce(f32[4,8,128]{2,1,0:T(8,128)S(1)} %fusion.70), channel_id=4, replica_groups=mesh['region'=8,'blk'=4] {'blk'}, use_global_device_ids=true, to_apply=%region_15.15.clone | all-reduce | flops 4096 | bytes 32768 | tf_op jit(solution)/shard_map/while
  186.1 6.4 all-reduce.14
  192.5 20.4 %all-reduce.15 = (f32[]{:T(128)}, f32[]{:T(128)}) all-reduce(f32[]{:T(128)} %get-tuple-element.277, f32[]{:T(128)} %get-tuple-element.278), channel_id=1, replica_groups=mesh['region'=8,'blk'=4] {'region'}, use_global_device_ids=true, to_apply=%region_13.13 | all-reduce | flops 2 | bytes 16 | tf_op jit(solution)/shard_map/while/body/eval_jaxpr/psum | solution.py:80
  230.2 5.4 fusion.68
  244.1 10.1 %all-reduce.13 = f32[4,8,128]{2,1,0:T(8,128)S(1)} all-reduce(f32[4,8,128]{2,1,0:T(8,128)S(1)} %fusion.70), channel_id=4, replica_groups=mesh['region'=8,'blk'=4] {'blk'}, use_global_device_ids=true, to_apply=%region_15.15.clone | all-reduce | flops 4096 | bytes 32768 | tf_op jit(solution)/shard_map/while
  255.4 6.4 all-reduce.14
  261.8 21.3 %all-reduce.15 = (f32[]{:T(128)}, f32[]{:T(128)}) all-reduce(f32[]{:T(128)} %get-tuple-element.277, f32[]{:T(128)} %get-tuple-element.278), channel_id=1, replica_groups=mesh['region'=8,'blk'=4] {'region'}, use_global_device_ids=true, to_apply=%region_13.13 | all-reduce | flops 2 | bytes 16 | tf_op jit(solution)/shard_map/while/body/eval_jaxpr/psum | solution.py:80
  300.4 5.4 fusion.68
  314.3 10.1 %all-reduce.13 = f32[4,8,128]{2,1,0:T(8,128)S(1)} all-reduce(f32[4,8,128]{2,1,0:T(8,128)S(1)} %fusion.70), channel_id=4, replica_groups=mesh['region'=8,'blk'=4] {'blk'}, use_global_device_ids=true, to_apply=%region_15.15.clone | all-reduce | flops 4096 | bytes 32768 | tf_op jit(solution)/shard_map/while
  325.6 6.4 all-reduce.14
  332.0 21.3 %all-reduce.15 = (f32[]{:T(128)}, f32[]{:T(128)}) all-reduce(f32[]{:T(128)} %get-tuple-element.277, f32[]{:T(128)} %get-tuple-element.278), channel_id=1, replica_groups=mesh['region'=8,'blk'=4] {'region'}, use_global_device_ids=true, to_apply=%region_13.13 | all-reduce | flops 2 | bytes 16 | tf_op jit(solution)/shard_map/while/body/eval_jaxpr/psum | solution.py:80
  370.5 5.4 fusion.68
  384.5 10.1 %all-reduce.13 = f32[4,8,128]{2,1,0:T(8,128)S(1)} all-reduce(f32[4,8,128]{2,1,0:T(8,128)S(1)} %fusion.70), channel_id=4, replica_groups=mesh['region'=8,'blk'=4] {'blk'}, use_global_device_ids=true, to_apply=%region_15.15.clone | all-reduce | flops 4096 | bytes 32768 | tf_op jit(solution)/shard_map/while
  395.8 6.4 all-reduce.14
  402.1 21.3 %all-reduce.15 = (f32[]{:T(128)}, f32[]{:T(128)}) all-reduce(f32[]{:T(128)} %get-tuple-element.277, f32[]{:T(128)} %get-tuple-element.278), channel_id=1, replica_groups=mesh['region'=8,'blk'=4] {'region'}, use_global_device_ids=true, to_apply=%region_13.13 | all-reduce | flops 2 | bytes 16 | tf_op jit(solution)/shard_map/while/body/eval_jaxpr/psum | solution.py:80
  440.8 5.4 fusion.68
  454.7 10.1 %all-reduce.13 = f32[4,8,128]{2,1,0:T(8,128)S(1)} all-reduce(f32[4,8,128]{2,1,0:T(8,128)S(1)} %fusion.70), channel_id=4, replica_groups=mesh['region'=8,'blk'=4] {'blk'}, use_global_device_ids=true, to_apply=%region_15.15.clone | all-reduce | flops 4096 | bytes 32768 | tf_op jit(solution)/shard_map/while
  466.0 6.4 all-reduce.14
  472.4 21.3 %all-reduce.15 = (f32[]{:T(128)}, f32[]{:T(128)}) all-reduce(f32[]{:T(128)} %get-tuple-element.277, f32[]{:T(128)} %get-tuple-element.278), channel_id=1, replica_groups=mesh['region'=8,'blk'=4] {'region'}, use_global_device_ids=true, to_apply=%region_13.13 | all-reduce | flops 2 | bytes 16 | tf_op jit(solution)/shard_map/while/body/eval_jaxpr/psum | solution.py:80
  525.0 10.1 %all-reduce.13 = f32[4,8,128]{2,1,0:T(8,128)S(1)} all-reduce(f32[4,8,128]{2,1,0:T(8,128)S(1)} %fusion.70), channel_id=4, replica_groups=mesh['region'=8,'blk'=4] {'blk'}, use_global_device_ids=true, to_apply=%region_15.15.clone | all-reduce | flops 4096 | bytes 32768 | tf_op jit(solution)/shard_map/while
  536.3 6.4 all-reduce.14
  542.6 21.3 %all-reduce.15 = (f32[]{:T(128)}, f32[]{:T(128)}) all-reduce(f32[]{:T(128)} %get-tuple-element.277, f32[]{:T(128)} %get-tuple-element.278), channel_id=1, replica_groups=mesh['region'=8,'blk'=4] {'region'}, use_global_device_ids=true, to_apply=%region_13.13 | all-reduce | flops 2 | bytes 16 | tf_op jit(solution)/shard_map/while/body/eval_jaxpr/psum | solution.py:80
  581.3 5.4 fusion.68
  595.2 10.1 %all-reduce.13 = f32[4,8,128]{2,1,0:T(8,128)S(1)} all-reduce(f32[4,8,128]{2,1,0:T(8,128)S(1)} %fusion.70), channel_id=4, replica_groups=mesh['region'=8,'blk'=4] {'blk'}, use_global_device_ids=true, to_apply=%region_15.15.clone | all-reduce | flops 4096 | bytes 32768 | tf_op jit(solution)/shard_map/while
  606.5 6.4 all-reduce.14
  612.9 21.3 %all-reduce.15 = (f32[]{:T(128)}, f32[]{:T(128)}) all-reduce(f32[]{:T(128)} %get-tuple-element.277, f32[]{:T(128)} %get-tuple-element.278), channel_id=1, replica_groups=mesh['region'=8,'blk'=4] {'region'}, use_global_device_ids=true, to_apply=%region_13.13 | all-reduce | flops 2 | bytes 16 | tf_op jit(solution)/shard_map/while/body/eval_jaxpr/psum | solution.py:80
  651.5 5.4 fusion.68
  665.5 10.1 %all-reduce.13 = f32[4,8,128]{2,1,0:T(8,128)S(1)} all-reduce(f32[4,8,128]{2,1,0:T(8,128)S(1)} %fusion.70), channel_id=4, replica_groups=mesh['region'=8,'blk'=4] {'blk'}, use_global_device_ids=true, to_apply=%region_15.15.clone | all-reduce | flops 4096 | bytes 32768 | tf_op jit(solution)/shard_map/while
  676.8 6.4 all-reduce.14
  683.1 21.3 %all-reduce.15 = (f32[]{:T(128)}, f32[]{:T(128)}) all-reduce(f32[]{:T(128)} %get-tuple-element.277, f32[]{:T(128)} %get-tuple-element.278), channel_id=1, replica_groups=mesh['region'=8,'blk'=4] {'region'}, use_global_device_ids=true, to_apply=%region_13.13 | all-reduce | flops 2 | bytes 16 | tf_op jit(solution)/shard_map/while/body/eval_jaxpr/psum | solution.py:80
  721.8 5.4 fusion.68
  735.7 10.1 %all-reduce.13 = f32[4,8,128]{2,1,0:T(8,128)S(1)} all-reduce(f32[4,8,128]{2,1,0:T(8,128)S(1)} %fusion.70), channel_id=4, replica_groups=mesh['region'=8,'blk'=4] {'blk'}, use_global_device_ids=true, to_apply=%region_15.15.clone | all-reduce | flops 4096 | bytes 32768 | tf_op jit(solution)/shard_map/while
  747.0 6.4 all-reduce.14
  753.4 21.3 %all-reduce.15 = (f32[]{:T(128)}, f32[]{:T(128)}) all-reduce(f32[]{:T(128)} %get-tuple-element.277, f32[]{:T(128)} %get-tuple-element.278), channel_id=1, replica_groups=mesh['region'=8,'blk'=4] {'region'}, use_global_device_ids=true, to_apply=%region_13.13 | all-reduce | flops 2 | bytes 16 | tf_op jit(solution)/shard_map/while/body/eval_jaxpr/psum | solution.py:80
  792.0 5.4 fusion.68
  806.0 10.1 %all-reduce.13 = f32[4,8,128]{2,1,0:T(8,128)S(1)} all-reduce(f32[4,8,128]{2,1,0:T(8,128)S(1)} %fusion.70), channel_id=4, replica_groups=mesh['region'=8,'blk'=4] {'blk'}, use_global_device_ids=true, to_apply=%region_15.15.clone | all-reduce | flops 4096 | bytes 32768 | tf_op jit(solution)/shard_map/while
  817.3 6.4 all-reduce.14
  823.6 21.3 %all-reduce.15 = (f32[]{:T(128)}, f32[]{:T(128)}) all-reduce(f32[]{:T(128)} %get-tuple-element.277, f32[]{:T(128)} %get-tuple-element.278), channel_id=1, replica_groups=mesh['region'=8,'blk'=4] {'region'}, use_global_device_ids=true, to_apply=%region_13.13 | all-reduce | flops 2 | bytes 16 | tf_op jit(solution)/shard_map/while/body/eval_jaxpr/psum | solution.py:80
  876.2 10.1 %all-reduce.13 = f32[4,8,128]{2,1,0:T(8,128)S(1)} all-reduce(f32[4,8,128]{2,1,0:T(8,128)S(1)} %fusion.70), channel_id=4, replica_groups=mesh['region'=8,'blk'=4] {'blk'}, use_global_device_ids=true, to_apply=%region_15.15.clone | all-reduce | flops 4096 | bytes 32768 | tf_op jit(solution)/shard_map/while
  887.5 6.4 all-reduce.14
  893.9 21.3 %all-reduce.15 = (f32[]{:T(128)}, f32[]{:T(128)}) all-reduce(f32[]{:T(128)} %get-tuple-element.277, f32[]{:T(128)} %get-tuple-element.278), channel_id=1, replica_groups=mesh['region'=8,'blk'=4] {'region'}, use_global_device_ids=true, to_apply=%region_13.13 | all-reduce | flops 2 | bytes 16 | tf_op jit(solution)/shard_map/while/body/eval_jaxpr/psum | solution.py:80
  (344 shorter events, 320.7 us)
Async XLA Ops:
  0.6 52.0 %all-to-all-start = ((f32[32,2,128,128]{3,2,1,0:T(8,128)}), f32[32,2,128,128]{3,2,1,0:T(8,128)}, u32[]{:S(2)}, u32[]{:S(2)}) async-start(f32[32,2,128,128]{3,2,1,0:T(8,128)} %param.7), calls=%async_computation | async-start | bytes 8388608 | tf_op jit(solution)/shard_map/all_to_all | solution.py:50
  60.2 4.7 collective-permute-start.4
  60.8 4.1 collective-permute-start.5
  80.9 4.4 collective-permute-start.6
  83.8 4.6 collective-permute-start.7
  97.4 4.7 collective-permute-start.8
  97.5 4.8 collective-permute-start.9
  153.6 4.6 collective-permute-start
  153.7 6.4 collective-permute-start.1
  169.0 4.7 collective-permute-start.2
  170.2 4.6 collective-permute-start.3
  221.1 6.2 collective-permute-start
  225.8 3.7 collective-permute-start.1
  238.5 4.5 collective-permute-start.2
  239.5 4.6 collective-permute-start.3
  291.3 6.2 collective-permute-start
  296.0 3.7 collective-permute-start.1
  308.7 4.5 collective-permute-start.2
  309.6 4.6 collective-permute-start.3
  361.5 6.2 collective-permute-start
  366.2 3.7 collective-permute-start.1
  378.9 4.5 collective-permute-start.2
  379.8 4.6 collective-permute-start.3
  431.7 6.2 collective-permute-start
  436.4 3.7 collective-permute-start.1
  449.1 4.5 collective-permute-start.2
  450.1 4.6 collective-permute-start.3
  502.0 6.2 collective-permute-start
  506.7 3.7 collective-permute-start.1
  519.4 4.5 collective-permute-start.2
  520.3 4.6 collective-permute-start.3
  572.2 6.2 collective-permute-start
  589.6 4.5 collective-permute-start.2
  590.6 4.6 collective-permute-start.3
  642.5 6.2 collective-permute-start
  647.2 3.7 collective-permute-start.1
  659.9 4.5 collective-permute-start.2
  660.8 4.6 collective-permute-start.3
  712.7 6.2 collective-permute-start
  730.1 4.5 collective-permute-start.2
  731.1 4.6 collective-permute-start.3
  783.0 6.2 collective-permute-start
  800.4 4.5 collective-permute-start.2
  801.3 4.6 collective-permute-start.3
  853.2 6.2 collective-permute-start
  857.9 3.7 collective-permute-start.1
  870.6 4.5 collective-permute-start.2
  871.6 4.6 collective-permute-start.3
  (23 other events, 137.2 us)
